TPU v7x, 128 devices: a whole 4x4x4 slice. The times are simulated.
128 devices in a mesh: path: 32 (over z_hi, y, x), tm: 4 (over z_lo, core).
Axes of the slice: x: 4, y: 4, z: 4 (z_hi: 2, z_lo: 2; z = z_hi * 2 + z_lo), core: 2. Of those that a mesh axis runs over, the one named last changes fastest.
Arguments:
- increments: bfloat16 [32768, 32, 1000], P(('path', 'tm')), may hold values from -6 to 6
- level_table: int32 [16384], replicated, may hold values from 0 to 4, as said below
- time_table: int32 [16384], replicated, may hold values from 0 to 31, as said below
Outputs:
- value_est: float32 [32], P('tm')
- grad_est: float32 [32, 1000], P('tm')
Inputs may be any that keep to these rules, and one draw needn't show every extreme that they name: `level_table`: never falls from one block to the next. `time_table`: split the 32 time points into as many runs of consecutive points as the tm axis has devices; the 128 consecutive entries of each device fall equally into every run.
All inputs are finite; a program needn't handle non-finite values.
Results may differ from a plain program's by a relative error of at most 0.0003.
The roundings to bfloat16 on the way count: a program that leaves them out, or rounds other values in their place, can miss the bound.
Values may be sent and summed in bfloat16 or wider, within the bound.
A program may use at most 128 MiB of HBM per device.

v0:
```python
import jax
import jax.numpy as jnp
from jax import lax
from jax.sharding import PartitionSpec as P

LEVELS = 5
BLOCK = 2
horizon = 0.3


def in_blocks(array, dim, peers):
    shape = array.shape
    blocks = array.reshape(*shape[:dim], peers, shape[dim] // peers, *shape[dim + 1 :])
    return jnp.moveaxis(blocks, dim, 0)


def sent_and_summed(array, axis, dim):
    blocks = in_blocks(array, dim, lax.axis_size(axis))
    arrived = lax.all_to_all(blocks, axis, split_axis=0, concat_axis=0, tiled=True)
    return arrived.sum(axis=0)


def copy_for_each(array, axis):
    peers = lax.axis_size(axis)
    return lax.all_to_all(
        jnp.broadcast_to(array[None], (peers, *array.shape)), axis, 0, 0, tiled=True
    )


def of_everyone(array, axis):
    return copy_for_each(array, axis).sum(axis=0)


def together(arrays, axis):
    vector, at, done = (jnp.concatenate([a.reshape(-1) for a in arrays]), 0, [])
    subtotal = of_everyone(vector, axis)
    for a in arrays:
        done.append(subtotal[at : at + a.size].reshape(a.shape))
        at += a.size
    return tuple(done)


def stride_weights(levels, starts, steps_k, step_len):
    steps = jnp.arange(steps_k)
    fine_stride = jnp.power(2, LEVELS - 1 - levels).astype(jnp.int32)
    coarse = fine_stride * 2
    live_steps = steps[None, :] >= starts[:, None]
    on_fine = steps[None, :] % fine_stride[:, None] == 0
    on_coarse = (steps[None, :] % coarse[:, None] == 0) & (levels[:, None] > 0)
    term = fine_stride[:, None] * on_fine.astype(jnp.int32) - coarse[:, None] * on_coarse.astype(
        jnp.int32
    )
    return step_len * (live_steps.astype(jnp.float32) * term.astype(jnp.float32))


def terminal(incr, starts):
    steps_k = incr.shape[1]
    width = incr.shape[2]
    step_len = horizon / steps_k
    steps = jnp.arange(steps_k)
    live_steps = (steps[None, :] >= starts[:, None]).astype(jnp.bfloat16)
    end_point = jnp.sqrt(step_len) * jnp.einsum(
        "pi,pid->pd", live_steps, incr, preferred_element_type=jnp.float32
    )
    remaining = horizon - starts.astype(jnp.float32) * step_len
    scaled = end_point / remaining[:, None]
    end_value = 1.0 / (2.0 + 0.4 * jnp.sum(end_point * end_point, axis=1) / width)
    return (scaled, end_value)


def partial_sums(path_total, scaled, row_index, path_share, row_count):
    select = (row_index[:, None] == jnp.arange(row_count)[None, :]).astype(jnp.float32)
    select = select * (path_share * path_total)[:, None]
    return (jnp.sum(select, axis=0), jnp.dot(select.T, scaled, precision=lax.Precision.HIGHEST))


def first_terms(incr, levels, starts, path_share, row_count, offset):
    scaled, end_value = terminal(incr, starts)
    path_total = end_value * (levels == 0).astype(jnp.float32)
    return partial_sums(path_total, scaled, starts - offset, path_share, row_count)


def second_terms(incr, levels, starts, path_share, value_one, grad_low, row_count, offset):
    paths, steps_k, width = incr.shape
    step_len = horizon / steps_k
    scaled, end_value = terminal(incr, starts)
    inner_dots = jnp.dot(
        incr.reshape(paths * steps_k, width), grad_low.T, preferred_element_type=jnp.float32
    ).reshape(paths, steps_k, steps_k)
    steps = jnp.arange(steps_k)
    window = (steps[None, :, None] >= starts[:, None, None]) & (
        steps[None, :, None] < steps[None, None, :]
    )
    estimate = value_one[None, :] + jnp.sqrt(step_len) * jnp.sum(
        inner_dots * window.astype(jnp.float32), axis=1
    )
    drift_term = estimate - estimate * estimate * estimate
    weights = stride_weights(levels, starts, steps_k, step_len)
    path_total = end_value * (levels == 0).astype(jnp.float32) + jnp.sum(
        weights * drift_term, axis=1
    )
    return partial_sums(path_total, scaled, starts - offset, path_share, row_count)


def shards(increments, level_table, time_table):
    groups = lax.axis_size("tm")
    devices = lax.axis_size("path") * groups
    my_index = lax.axis_index("path") * groups + lax.axis_index("tm")
    blk_dev = level_table.shape[0] // devices
    steps_k = increments.shape[1]
    lvl_hot = (level_table[:, None] == jnp.arange(LEVELS)[None, :]).astype(jnp.float32)
    time_hot = (time_table[:, None] == jnp.arange(steps_k)[None, :]).astype(jnp.float32)
    counts = jnp.dot(lvl_hot.T, time_hot, precision=lax.Precision.HIGHEST)
    own_levels = lax.dynamic_slice_in_dim(level_table, my_index * blk_dev, blk_dev)
    own_times = lax.dynamic_slice_in_dim(time_table, my_index * blk_dev, blk_dev)
    lvl_path = jnp.repeat(own_levels, BLOCK)
    time_path = jnp.repeat(own_times, BLOCK)
    path_share = 1.0 / (BLOCK * counts[lvl_path, time_path])
    value_one, grad_one = lax.psum(
        first_terms(increments, lvl_path, time_path, path_share, steps_k, 0), ("path", "tm")
    )
    grad_low = grad_one.astype(jnp.bfloat16)
    value_part, grad_part = jax.tree.map(
        lambda part: sent_and_summed(part, "tm", 0),
        second_terms(increments, lvl_path, time_path, path_share, value_one, grad_low, steps_k, 0),
    )
    value_est, grad_est = together((value_part, grad_part), "path")
    return (value_est, grad_est)


def solution(mesh):
    placed = (P(("path", "tm"), None, None), P(), P())
    return jax.shard_map(
        shards, mesh=mesh, in_specs=placed, out_specs=(P("tm"), P("tm", None)), check_vma=False
    )
```

profile of v0, /device:TPU:0, one launch (start us, length us, event | category | flops | bytes accessed | tf_op | source)
XLA Modules:
  0.0 166.2 jit_solution(9377580538771082591)
XLA Ops:
  0.6 0.8 broadcast_compare_fusion
  1.4 0.8 dynamic_slice.6
  2.2 1.4 fusion
  4.3 23.5 %copy.17 = bf16[256,32,1000]{2,1,0:T(8,128)(2,1)} copy(bf16[256,32,1000]{0,2,1:T(8,128)(2,1)} %param.5) | data formatting | bytes 32768000 | tf_op args[0]
  27.7 7.1 %multiply_reduce_fusion = f32[256,1000]{0,1:T(8,128)S(1)} fusion(bf16[256,32,1000]{0,2,1:T(8,128)(2,1)} %param.5, f32[256,32]{0,1:T(8,128)S(1)} %get-tuple-element.16), kind=kLoop, calls=%fused_computation.1 | loop fusion | flops 24320000 | bytes 17440768 | tf_op jit(solution)/shard_map/pi,pid->pd/dot_general | solution.py:62
  34.8 0.2 multiply_reduce_fusion.1
  35.2 1.4 gather_fusion
  36.8 1.0 fusion.2
  37.7 69.1 %all-reduce = (bf16[32,1000]{1,0:T(8,128)(2,1)S(1)}, f32[32]{0:T(128)S(1)}) all-reduce(f32[32,1000]{1,0:T(8,128)S(1)} %fusion.2, f32[32]{0:T(128)S(1)} %select_reduce_fusion.2), channel_id=1, replica_groups=mesh['path'=32,'tm'=4] {'path','tm'}, use_global_device_ids=true, to_apply=%region_3.5 | all-reduce | flops 32032 | bytes 192256 | tf_op jit(solution)/shard_map/psum | solution.py:119
  106.8 10.7 %convolution_bitcast_fusion = f32[8192,32]{0,1:T(8,128)S(1)} fusion(bf16[8192,1000]{1,0:T(8,128)(2,1)} %bitcast.13, bf16[32,1000]{1,0:T(8,128)(2,1)S(1)} %get-tuple-element.3), kind=kOutput, calls=%fused_computation.2 | convolution fusion | flops 524288000 | bytes 17496576 | tf_op jit(solution)/shard_map/dot_general | solution.py:87
  117.5 2.7 %reshape.304 = f32[256,32,32]{1,0,2:T(8,128)} reshape(f32[8192,32]{0,1:T(8,128)S(1)} %convolution_bitcast_fusion) | data formatting | bytes 2097152 | tf_op jit(solution)/shard_map/reshape | solution.py:89
  122.0 3.3 %select_reduce_fusion = f32[256,32]{0,1:T(8,128)S(1)} fusion(f32[256,32,32]{1,0,2:T(8,128)} %reshape.304, pred[32,32]{0,1:T(8,128)(4,1)S(1)} %iota_compare_fusion.8, pred[256,32]{1,0:T(8,128)(4,1)S(1)} %copy.16), kind=kLoop, calls=%fused_computation.3 | loop fusion | flops 778240 | bytes 1090560 | tf_op jit(solution)/shard_map/reduce_sum | solution.py:94
  125.4 0.7 fusion.8
  126.2 0.7 all_to_all.13
  126.9 3.4 %all-to-all-start = ((f32[4,1,8]{2,1,0:T(1,128)}), f32[4,1,8]{2,1,0:T(1,128)S(1)}, u32[]{:S(2)}, u32[]{:S(2)}) async-start(f32[4,1,8]{2,1,0:T(1,128)} %bitcast.5), calls=%async_computation | async-start | bytes 4096 | tf_op jit(solution)/shard_map/all_to_all | solution.py:19
  130.3 1.6 convolution_bitcast_fusion.1
  131.9 1.9 %all-to-all-done = f32[4,1,8]{2,1,0:T(1,128)S(1)} async-done(((f32[4,1,8]{2,1,0:T(1,128)}), f32[4,1,8]{2,1,0:T(1,128)S(1)}, u32[]{:S(2)}, u32[]{:S(2)}) %all-to-all-start) | async-done | bytes 160 | tf_op jit(solution)/shard_map/all_to_all | solution.py:19
  133.8 3.3 %all-to-all-start.1 = ((f32[4,8,1000]{2,1,0:T(8,128)}), f32[4,8,1000]{2,1,0:T(8,128)S(1)}, u32[]{:S(2)}, u32[]{:S(2)}) async-start(f32[4,8,1000]{2,1,0:T(8,128)} %convolution_bitcast_fusion.1), calls=%async_computation.1 | async-start | bytes 262144 | tf_op jit(solution)/shard_map/all_to_all | solution.py:19
  137.2 4.5 %all-to-all-done.1 = f32[4,8,1000]{2,1,0:T(8,128)S(1)} async-done(((f32[4,8,1000]{2,1,0:T(8,128)}), f32[4,8,1000]{2,1,0:T(8,128)S(1)}, u32[]{:S(2)}, u32[]{:S(2)}) %all-to-all-start.1) | async-done | bytes 128032 | tf_op jit(solution)/shard_map/all_to_all | solution.py:19
  141.9 0.5 broadcast_in_dim.33
  142.4 21.9 %all_to_all.20 = f32[32,1,8008]{2,1,0:T(1,128)S(1)} all-to-all(f32[32,1,8008]{2,1,0:T(1,128)S(1)} %broadcast_in_dim.33), channel_id=1, replica_groups=mesh['path'=32,'tm'=4] {'path'}, dimensions={0} | all-to-all | bytes 2050048 | tf_op jit(solution)/shard_map/all_to_all | solution.py:25
  164.3 0.6 reduce_sum.83
  165.0 0.5 slice.10
  165.5 0.7 reshape.307
  (41 shorter events, 3.2 us)
Async XLA Ops:
  126.9 6.9 %all-to-all-start = ((f32[4,1,8]{2,1,0:T(1,128)}), f32[4,1,8]{2,1,0:T(1,128)S(1)}, u32[]{:S(2)}, u32[]{:S(2)}) async-start(f32[4,1,8]{2,1,0:T(1,128)} %bitcast.5), calls=%async_computation | async-start | bytes 4096 | tf_op jit(solution)/shard_map/all_to_all | solution.py:19
  133.8 7.9 %all-to-all-start.1 = ((f32[4,8,1000]{2,1,0:T(8,128)}), f32[4,8,1000]{2,1,0:T(8,128)S(1)}, u32[]{:S(2)}, u32[]{:S(2)}) async-start(f32[4,8,1000]{2,1,0:T(8,128)} %convolution_bitcast_fusion.1), calls=%async_computation.1 | async-start | bytes 262144 | tf_op jit(solution)/shard_map/all_to_all | solution.py:19
where the time goes:
time: 167 us; the launch traced here: 166 us
  blocking collectives  91 us (54%)
  local copies, waits for them, and re-layouts  33.5 us (20%)
  matrix products  14.6 us (9%)
  other arithmetic  13.1 us (8%)
  starting transfers between devices  6.73 us (4%)
  waiting for transfers between devices  6.41 us (4%)
    psum x1, blocking collectives, shards(): lax.psum(first_terms(increments, lvl_path, time_path, path_share, steps_k...  69.1 us
    unnamed x1, local copies, waits for them, and re-layouts  23.5 us
    all_to_all x1, blocking collectives, copy_for_each(): lax.all_to_all(jnp.broadcast_to(array[None], (peers, *array.shape)), axis...  21.9 us
    dot_general x1, matrix products, second_terms(): jnp.dot(incr.reshape(paths * steps_k, width), grad_low.T, preferred_eleme...  10.7 us
    dot_general x1, other arithmetic, terminal(): jnp.einsum('pi,pid->pd', live_steps, incr, preferred_element_type=jnp.flo...  7.07 us
    all_to_all x2, starting transfers between devices, sent_and_summed(): lax.all_to_all(blocks, axis, split_axis=0, concat_axis=0, tiled=True)  6.73 us
    all_to_all x2, waiting for transfers between devices, sent_and_summed(): lax.all_to_all(blocks, axis, split_axis=0, concat_axis=0, tiled=True)  6.41 us
    reduce_sum x1, other arithmetic, second_terms(): jnp.sum(inner_dots * window.astype(jnp.float32), axis=1)  3.35 us
  transfers between devices with their start and end apart: 2, of which 2 were waited for; matrix products, arithmetic and copies ran while one was open for 1% of the time, Pallas kernels for 0%

commit v1 on v0

--- a/solution.py
+++ b/solution.py
@@ -117,7 +117,7 @@
     time_path = jnp.repeat(own_times, BLOCK)
     path_share = 1.0 / (BLOCK * counts[lvl_path, time_path])
     value_one, grad_one = lax.psum(
-        first_terms(increments, lvl_path, time_path, path_share, steps_k, 0), ("path", "tm")
+        lax.psum(first_terms(increments, lvl_path, time_path, path_share, steps_k, 0), "tm"), "path"
     )
     grad_low = grad_one.astype(jnp.bfloat16)
     value_part, grad_part = jax.tree.map(

time: 167 us -> 309 us (1.85)
  blocking collectives: 91 us -> 213 us
  between operations: 0.86 us -> 14.2 us
  waiting for transfers between devices: 6.41 us -> 12 us
    psum x0 -> x1, blocking collectives: none -> 185 us  [shards(): lax.psum(lax.psum(first_terms(increments, lvl_path, time_path, path_share...]
    psum x1, blocking collectives: 69.1 us -> 7.45 us  [shards(): lax.psum(first_terms(increments, lvl_path, time_path, path_share, steps_k...]
    psum x0 -> x1, waiting for transfers between devices: none -> 5.55 us  [shards(): lax.psum(first_terms(increments, lvl_path, time_path, path_share, steps_k...]
  transfers between devices with their start and end apart: 2 -> 3, of which waited for: 2 -> 3; matrix products, arithmetic and copies ran while one was open for 1% -> 9% of each run, Pallas kernels for 0% -> 0%
where the time goes in v1:
time: 309 us; the launch traced here: 308 us
  blocking collectives  213 us (69%)
  local copies, waits for them, and re-layouts  33.5 us (11%)
  matrix products  15.3 us (5%)
  between operations  14.2 us (5%)
  other arithmetic  13.1 us (4%)
  waiting for transfers between devices  12 us (4%)
  starting transfers between devices  6.76 us (2%)
    psum x1, blocking collectives, shards(): lax.psum(lax.psum(first_terms(increments, lvl_path, time_path, path_share...  185 us
    unnamed x1, local copies, waits for them, and re-layouts  23.5 us
    all_to_all x1, blocking collectives, copy_for_each(): lax.all_to_all(jnp.broadcast_to(array[None], (peers, *array.shape)), axis...  21 us
    dot_general x1, matrix products, second_terms(): jnp.dot(incr.reshape(paths * steps_k, width), grad_low.T, preferred_eleme...  10.7 us
    psum x1, blocking collectives, shards(): lax.psum(first_terms(increments, lvl_path, time_path, path_share, steps_k...  7.45 us
    dot_general x1, other arithmetic, terminal(): jnp.einsum('pi,pid->pd', live_steps, incr, preferred_element_type=jnp.flo...  7.07 us
    all_to_all x2, starting transfers between devices, sent_and_summed(): lax.all_to_all(blocks, axis, split_axis=0, concat_axis=0, tiled=True)  6.73 us
    all_to_all x2, waiting for transfers between devices, sent_and_summed(): lax.all_to_all(blocks, axis, split_axis=0, concat_axis=0, tiled=True)  6.41 us
  transfers between devices with their start and end apart: 3, of which 3 were waited for; matrix products, arithmetic and copies ran while one was open for 9% of the time, Pallas kernels for 0%

profile of v1, /device:TPU:0, one launch (start us, length us, event | category | flops | bytes accessed | tf_op | source)
XLA Modules:
  0.0 308.2 jit_solution(17331271535098273233)
XLA Ops:
  7.2 0.8 broadcast_compare_fusion
  8.0 0.8 dynamic_slice.6
  8.7 1.4 fusion
  10.7 7.1 %multiply_reduce_fusion = f32[256,1000]{0,1:T(8,128)S(1)} fusion(bf16[256,32,1000]{0,2,1:T(8,128)(2,1)} %param.5, f32[256,32]{0,1:T(8,128)S(1)} %get-tuple-element.16), kind=kLoop, calls=%fused_computation.1 | loop fusion | flops 24320000 | bytes 17440768 | tf_op jit(solution)/shard_map/pi,pid->pd/dot_general | solution.py:62
  18.3 1.4 gather_fusion
  19.7 1.6 fusion.2
  23.0 23.5 %copy.17 = bf16[256,32,1000]{2,1,0:T(8,128)(2,1)} copy(bf16[256,32,1000]{0,2,1:T(8,128)(2,1)} %param.5) | data formatting | bytes 32768000 | tf_op args[0]
  46.9 7.4 %psum.28 = f32[32]{0:T(128)S(1)} all-reduce(f32[32]{0:T(128)S(1)} %select_reduce_fusion.2), channel_id=1, replica_groups=mesh['path'=32,'tm'=4] {'tm'}, use_global_device_ids=true, to_apply=%region_2.4 | all-reduce | flops 32 | bytes 256 | tf_op jit(solution)/shard_map/psum | solution.py:120
  54.3 5.6 %all-reduce.3.cloned.1.call-done = f32[32,1000]{1,0:T(8,128)} async-done(((f32[32,1000]{1,0:T(8,128)}), f32[32,1000]{1,0:T(8,128)}) %all-reduce.3.cloned.1.call-update) | async-done | bytes 128016 | tf_op jit(solution)/shard_map/psum | solution.py:120
  59.9 184.8 %all-reduce = (bf16[32,1000]{1,0:T(8,128)(2,1)S(1)}, f32[32]{0:T(128)S(1)}) all-reduce(f32[32,1000]{1,0:T(8,128)} %all-reduce.3.cloned.1.call-done, f32[32]{0:T(128)S(1)} %psum.28), channel_id=1, replica_groups=mesh['path'=32,'tm'=4] {'path'}, use_global_device_ids=true, to_apply=%region_5.7 | all-reduce | flops 32032 | bytes 192256 | tf_op jit(solution)/shard_map/psum | solution.py:119
  244.7 10.7 %convolution_bitcast_fusion = f32[8192,32]{0,1:T(8,128)S(1)} fusion(bf16[8192,1000]{1,0:T(8,128)(2,1)} %bitcast.13, bf16[32,1000]{1,0:T(8,128)(2,1)S(1)} %get-tuple-element.3), kind=kOutput, calls=%fused_computation.2 | convolution fusion | flops 524288000 | bytes 17496576 | tf_op jit(solution)/shard_map/dot_general | solution.py:87
  255.4 2.7 reshape.304
  258.1 3.3 %select_reduce_fusion = f32[256,32]{0,1:T(8,128)S(1)} fusion(f32[256,32,32]{1,0,2:T(8,128)} %reshape.304, pred[32,32]{0,1:T(8,128)(4,1)S(1)} %iota_compare_fusion.8, pred[256,32]{1,0:T(8,128)(4,1)S(1)} %copy.16), kind=kLoop, calls=%fused_computation.3 | loop fusion | flops 778240 | bytes 1090560 | tf_op jit(solution)/shard_map/reduce_sum | solution.py:94
  261.4 0.7 fusion.8
  262.3 0.7 all_to_all.13
  262.9 3.4 %all-to-all-start = ((f32[4,1,8]{2,1,0:T(1,128)}), f32[4,1,8]{2,1,0:T(1,128)S(1)}, u32[]{:S(2)}, u32[]{:S(2)}) async-start(f32[4,1,8]{2,1,0:T(1,128)} %bitcast.5), calls=%async_computation | async-start | bytes 4096 | tf_op jit(solution)/shard_map/all_to_all | solution.py:19
  266.3 1.6 convolution_bitcast_fusion.1
  268.0 1.9 all-to-all-done
  269.8 3.3 %all-to-all-start.1 = ((f32[4,8,1000]{2,1,0:T(8,128)}), f32[4,8,1000]{2,1,0:T(8,128)S(1)}, u32[]{:S(2)}, u32[]{:S(2)}) async-start(f32[4,8,1000]{2,1,0:T(8,128)} %convolution_bitcast_fusion.1), calls=%async_computation.1 | async-start | bytes 262144 | tf_op jit(solution)/shard_map/all_to_all | solution.py:19
  273.2 4.5 %all-to-all-done.1 = f32[4,8,1000]{2,1,0:T(8,128)S(1)} async-done(((f32[4,8,1000]{2,1,0:T(8,128)}), f32[4,8,1000]{2,1,0:T(8,128)S(1)}, u32[]{:S(2)}, u32[]{:S(2)}) %all-to-all-start.1) | async-done | bytes 128032 | tf_op jit(solution)/shard_map/all_to_all | solution.py:19
  277.9 0.5 broadcast_in_dim.33
  278.4 21.0 %all_to_all.20 = f32[32,1,8008]{2,1,0:T(1,128)S(1)} all-to-all(f32[32,1,8008]{2,1,0:T(1,128)S(1)} %broadcast_in_dim.33), channel_id=1, replica_groups=mesh['path'=32,'tm'=4] {'path'}, dimensions={0} | all-to-all | bytes 2050048 | tf_op jit(solution)/shard_map/all_to_all | solution.py:25
  299.5 0.6 reduce_sum.83
  300.7 0.7 reshape.307
  (46 shorter events, 4.0 us)
Async XLA Ops:
  7.2 52.7 %all-reduce.3.cloned.1.call-start = ((), (), s32[]{:S(2)}) async-start(), calls=%async_computation.3 | async-start | bytes 262144 | tf_op jit(solution)/shard_map/psum | solution.py:120
  262.9 6.9 %all-to-all-start = ((f32[4,1,8]{2,1,0:T(1,128)}), f32[4,1,8]{2,1,0:T(1,128)S(1)}, u32[]{:S(2)}, u32[]{:S(2)}) async-start(f32[4,1,8]{2,1,0:T(1,128)} %bitcast.5), calls=%async_computation | async-start | bytes 4096 | tf_op jit(solution)/shard_map/all_to_all | solution.py:19
  269.8 7.9 %all-to-all-start.1 = ((f32[4,8,1000]{2,1,0:T(8,128)}), f32[4,8,1000]{2,1,0:T(8,128)S(1)}, u32[]{:S(2)}, u32[]{:S(2)}) async-start(f32[4,8,1000]{2,1,0:T(8,128)} %convolution_bitcast_fusion.1), calls=%async_computation.1 | async-start | bytes 262144 | tf_op jit(solution)/shard_map/all_to_all | solution.py:19
Sparse Core Ops, SparseCore 0:
  21.5 38.3 all-reduce.2
